TPU v7x, 32 devices: a whole 2x2x4 slice. The times are simulated.
32 devices in a mesh: seq: 16 (over z, y, x), blk: 2 (over core).
Axes of the slice: x: 2, y: 2, z: 4, core: 2. Of those that a mesh axis runs over, the one named last changes fastest.
Arguments:
- query: bfloat16 [2048, 5120], P(('blk', 'seq')), may hold values from -139 to 139
- keys: bfloat16 [2048, 5120], P(('blk', 'seq')), may hold values from -4.5 to 4.5
- values: bfloat16 [2048, 5120], P(('blk', 'seq')), may hold values from -6 to 6
Outputs:
- attended: bfloat16 [2048, 5120], P(('blk', 'seq'))
All inputs are finite; a program needn't handle non-finite values.
Results may differ from a plain program's by a relative error of at most 0.008.
Values may be sent and summed in bfloat16 or wider, within the bound.
No kernel may reach another device: no remote copies, remote signals or barrier semaphores. Data moves between devices by JAX's collectives and lax.ppermute only.
A program may use at most 64 MiB of HBM per device.

v0:
```python
import jax
import jax.numpy as jnp
from jax import lax
from jax.sharding import PartitionSpec as P

HEADS = 40


def partner(value, axis, bit):
    mask = 2**bit
    pairs = [(source, source ^ mask) for source in range(lax.axis_size(axis))]
    return lax.ppermute(value, axis, pairs)


def partial_block(q_rows, k_tile, v_tile):
    scores = lax.dot_general(
        q_rows, k_tile, (((1,), (1,)), ((), ())), preferred_element_type=jnp.float32
    ) * q_rows.shape[1] ** (-0.5)
    peak = jnp.max(scores, axis=1)
    expo = jnp.exp(scores - peak[:, None])
    totals = jnp.sum(expo, axis=1)
    summed = jnp.dot(expo.astype(jnp.bfloat16), v_tile, preferred_element_type=jnp.float32)
    return (peak, totals, summed)


def combine_parts(left, right):
    peak = jnp.maximum(left[0], right[0])
    scale_left = jnp.exp(left[0] - peak)
    scale_right = jnp.exp(right[0] - peak)
    totals = scale_left * left[1] + scale_right * right[1]
    summed = scale_left[:, None] * left[2] + scale_right[:, None] * right[2]
    return (peak, totals, summed)


def attend_rows(q_rows, first_k, first_v, second_k, second_v):
    state = partial_block(q_rows, first_k, first_v)
    state = combine_parts(state, partial_block(q_rows, second_k, second_v))
    return (state[2] / state[1][:, None]).astype(jnp.bfloat16)


def attend_item(args):
    q_head, first_k, first_v, second_k, second_v = args
    length, width = q_head.shape
    rows = min(512, length)

    def block(q_rows):
        return attend_rows(q_rows, first_k, first_v, second_k, second_v)

    return lax.map(block, q_head.reshape(length // rows, rows, width)).reshape(length, width)


def items_first(array):
    return jnp.transpose(array.reshape(array.shape[0], array.shape[2], array.shape[3]), (1, 0, 2))


def attend_items(pieces):
    q_group, k_group, v_group = pieces
    q_heads = items_first(q_group)
    k_heads = items_first(k_group)
    v_heads = items_first(v_group)
    stacked = jnp.stack([k_heads, v_heads])
    other = partner(stacked, "blk", 0)
    tiles = (q_heads, k_heads, v_heads, other[0], other[1])
    outcome = lax.map(attend_item, tiles)
    count, length, width = outcome.shape
    outcome = jnp.transpose(outcome, (1, 0, 2)).reshape(length, 1, count, width)
    return lax.all_to_all(outcome, "seq", split_axis=0, concat_axis=1, tiled=True)


def on_device(query, keys, values):
    groups = lax.axis_size("seq")
    width = query.shape[1] // HEADS
    tok_rows = query.shape[0]
    key_source, value_source = (keys, values)
    per_dev = (HEADS + groups - 1) // groups
    slots_all = per_dev * groups

    def split_heads(array):
        count_rows = array.shape[0]
        shaped = array.reshape(count_rows, HEADS, width)
        shaped = jnp.pad(shaped, ((0, 0), (0, slots_all - HEADS), (0, 0)))
        return shaped.reshape(count_rows, groups, per_dev, width)

    result = attend_items(
        (
            lax.all_to_all(split_heads(query), "seq", split_axis=1, concat_axis=0, tiled=True),
            lax.all_to_all(split_heads(key_source), "seq", split_axis=1, concat_axis=0, tiled=True),
            lax.all_to_all(
                split_heads(value_source), "seq", split_axis=1, concat_axis=0, tiled=True
            ),
        )
    )
    result = result.reshape(tok_rows, slots_all, width)[:, :HEADS]
    return result.reshape(tok_rows, HEADS * width)


def solution(mesh):
    placed = (P(("blk", "seq"), None), P(("blk", "seq"), None), P(("blk", "seq"), None))
    return jax.shard_map(
        on_device, mesh=mesh, in_specs=placed, out_specs=P(("blk", "seq"), None), check_vma=False
    )
```

profile of v0, /device:TPU:0, one launch (start us, length us, event | category | flops | bytes accessed | tf_op | source)
XLA Modules:
  0.0 155.3 jit_solution(6471587082868300585)
XLA Ops:
  0.0 1.1 copy-done
  1.3 1.0 pad.11.clone
  2.2 8.3 %all-to-all-start.1 = ((bf16[64,16,3,128]{3,0,2,1:T(8,128)(2,1)}), bf16[64,16,3,128]{3,0,2,1:T(8,128)(2,1)S(1)}, u32[]{:S(2)}, u32[]{:S(2)}) async-start(bf16[64,16,3,128]{3,0,2,1:T(8,128)(2,1)} %bitcast.13), calls=%async_computation.1 | async-start | bytes 1572864 | tf_op jit(solution)/shard_map/all_to_all | solution.py:87
  10.8 1.0 pad.12.clone
  11.8 18.5 %all-to-all-done.1 = bf16[64,16,3,128]{3,0,2,1:T(8,128)(2,1)S(1)} async-done(((bf16[64,16,3,128]{3,0,2,1:T(8,128)(2,1)}), bf16[64,16,3,128]{3,0,2,1:T(8,128)(2,1)S(1)}, u32[]{:S(2)}, u32[]{:S(2)}) %all-to-all-start.1) | async-done | bytes 786464 | tf_op jit(solution)/shard_map/all_to_all | solution.py:87
  30.3 5.0 %all-to-all-start.2 = ((bf16[64,16,3,128]{3,0,2,1:T(8,128)(2,1)}), bf16[64,16,3,128]{3,0,2,1:T(8,128)(2,1)S(1)}, u32[]{:S(2)}, u32[]{:S(2)}) async-start(bf16[64,16,3,128]{3,0,2,1:T(8,128)(2,1)} %bitcast.18), calls=%async_computation.2 | async-start | bytes 1572864 | tf_op jit(solution)/shard_map/all_to_all | solution.py:88
  35.3 18.6 %all-to-all-done.2 = bf16[64,16,3,128]{3,0,2,1:T(8,128)(2,1)S(1)} async-done(((bf16[64,16,3,128]{3,0,2,1:T(8,128)(2,1)}), bf16[64,16,3,128]{3,0,2,1:T(8,128)(2,1)S(1)}, u32[]{:S(2)}, u32[]{:S(2)}) %all-to-all-start.2) | async-done | bytes 786464 | tf_op jit(solution)/shard_map/all_to_all | solution.py:88
  53.9 0.9 copy-done.2
  54.8 1.3 copy.18
  56.0 1.3 pad_maximum_fusion
  57.5 1.0 pad.10.clone
  58.5 5.0 %all-to-all-start = ((bf16[64,16,3,128]{3,0,2,1:T(8,128)(2,1)}), bf16[64,16,3,128]{3,0,2,1:T(8,128)(2,1)S(1)}, u32[]{:S(2)}, u32[]{:S(2)}) async-start(bf16[64,16,3,128]{3,0,2,1:T(8,128)(2,1)} %bitcast.121), calls=%async_computation | async-start | bytes 1572864 | tf_op jit(solution)/shard_map/all_to_all | solution.py:86
  63.4 20.1 %all-to-all-done = bf16[64,16,3,128]{3,0,2,1:T(8,128)(2,1)S(1)} async-done(((bf16[64,16,3,128]{3,0,2,1:T(8,128)(2,1)}), bf16[64,16,3,128]{3,0,2,1:T(8,128)(2,1)S(1)}, u32[]{:S(2)}, u32[]{:S(2)}) %all-to-all-start) | async-done | bytes 786464 | tf_op jit(solution)/shard_map/all_to_all | solution.py:86
  83.5 0.9 copy.14
  84.5 2.6 %slice_bitcast_fusion = (bf16[3,1024,128]{2,1,0:T(8,128)(2,1)}, bf16[3,1024,128]{2,1,0:T(8,128)(2,1)}) fusion(bf16[2,3,1024,128]{3,2,1,0:T(8,128)(2,1)} %collective-permute-done), kind=kLoop, calls=%fused_computation.42 | loop fusion | bytes 3145728 | tf_op jit(solution)/shard_map/squeeze | solution.py:63
  87.1 34.5 %while.21 = (s32[]{:T(128)}, bf16[3,1024,128]{2,1,0:T(8,128)(2,1)}, bf16[3,1024,128]{2,1,0:T(8,128)(2,1)}, bf16[3,1024,128]{2,1,0:T(8,128)(2,1)S(1)}, bf16[3,102...) while((s32[]{:T(128)}, bf16[3,1024,128]{2,1,0:T(8,128)(2,1)}, ...), condition=%wide.region_7.8_spmd, body=%wide.region_0.7_spmd.sunk | while | flops 545588224 | bytes 18780980 | solution.py:64
  87.1 1.0 dynamic-slice_bitcast_fusion.6
  88.1 1.7 %dynamic-slice_bitcast_fusion.7 = (bf16[1024,128]{1,0:T(8,128)(2,1)}, bf16[1024,128]{1,0:T(8,128)(2,1)S(1)}) fusion(bf16[3,1024,128]{2,1,0:T(8,128)(2,1)} %get-tuple-element.302, s32[]{:T(128)} %get-tuple-element.286, bf16[3,1024,128]{2,1,0:T(8,128)(2,1)S(1)} %get-tuple-element.300), kind=kLoop, calls=%fused_computation.35.clone.1 | loop fusion | bytes 1048580 | tf_op jit(solution)/shard_map/while/body/jit(dynamic_index_in_dim)/squeeze | solution.py:64
  89.8 1.0 constant_dynamic-slice_fusion.2
  90.8 7.1 %while.22 = (s32[]{:T(128)}, bf16[2,512,128]{2,1,0:T(8,128)(2,1)S(1)}, bf16[2,512,128]{2,1,0:T(8,128)(2,1)S(1)}, bf16[1024,128]{1,0:T(8,128)(2,1)S(1)}, bf16[102...) while((s32[]{:T(128)}, ...), condition=%wide.region_6.6_spmd, body=%wide.region_1.5_spmd.sunk | while | flops 545588224 | bytes 15634557 | solution.py:49
  90.8 0.5 multiply_reduce_fusion.4
  91.3 0.5 multiply_reduce_fusion.5
  91.8 1.0 fusion.50
  92.8 0.5 convolution_multiply_fusion.3
  93.7 0.6 fusion.51
  94.3 0.5 multiply_reduce_fusion.4
  94.9 0.5 multiply_reduce_fusion.5
  95.4 1.0 fusion.50
  96.4 0.5 convolution_multiply_fusion.3
  97.3 0.6 fusion.51
  97.9 0.7 bitcast_dynamic-update-slice_fusion.2
  98.6 1.0 dynamic-slice_bitcast_fusion.6
  99.6 1.7 %dynamic-slice_bitcast_fusion.7 = (bf16[1024,128]{1,0:T(8,128)(2,1)}, bf16[1024,128]{1,0:T(8,128)(2,1)S(1)}) fusion(bf16[3,1024,128]{2,1,0:T(8,128)(2,1)} %get-tuple-element.302, s32[]{:T(128)} %get-tuple-element.286, bf16[3,1024,128]{2,1,0:T(8,128)(2,1)S(1)} %get-tuple-element.300), kind=kLoop, calls=%fused_computation.35.clone.1 | loop fusion | bytes 1048580 | tf_op jit(solution)/shard_map/while/body/jit(dynamic_index_in_dim)/squeeze | solution.py:64
  101.3 1.0 constant_dynamic-slice_fusion.2
  102.3 7.1 %while.22 = (s32[]{:T(128)}, bf16[2,512,128]{2,1,0:T(8,128)(2,1)S(1)}, bf16[2,512,128]{2,1,0:T(8,128)(2,1)S(1)}, bf16[1024,128]{1,0:T(8,128)(2,1)S(1)}, bf16[102...) while((s32[]{:T(128)}, ...), condition=%wide.region_6.6_spmd, body=%wide.region_1.5_spmd.sunk | while | flops 545588224 | bytes 15634557 | solution.py:49
  102.3 0.5 multiply_reduce_fusion.4
  102.8 0.5 multiply_reduce_fusion.5
  103.3 1.0 fusion.50
  104.3 0.5 convolution_multiply_fusion.3
  105.2 0.6 fusion.51
  105.8 0.5 multiply_reduce_fusion.4
  106.3 0.5 multiply_reduce_fusion.5
  106.9 1.0 fusion.50
  107.8 0.5 convolution_multiply_fusion.3
  108.8 0.6 fusion.51
  109.4 0.7 bitcast_dynamic-update-slice_fusion.2
  110.1 1.0 dynamic-slice_bitcast_fusion.6
  111.1 1.7 %dynamic-slice_bitcast_fusion.7 = (bf16[1024,128]{1,0:T(8,128)(2,1)}, bf16[1024,128]{1,0:T(8,128)(2,1)S(1)}) fusion(bf16[3,1024,128]{2,1,0:T(8,128)(2,1)} %get-tuple-element.302, s32[]{:T(128)} %get-tuple-element.286, bf16[3,1024,128]{2,1,0:T(8,128)(2,1)S(1)} %get-tuple-element.300), kind=kLoop, calls=%fused_computation.35.clone.1 | loop fusion | bytes 1048580 | tf_op jit(solution)/shard_map/while/body/jit(dynamic_index_in_dim)/squeeze | solution.py:64
  112.8 1.0 constant_dynamic-slice_fusion.2
  113.8 7.1 %while.22 = (s32[]{:T(128)}, bf16[2,512,128]{2,1,0:T(8,128)(2,1)S(1)}, bf16[2,512,128]{2,1,0:T(8,128)(2,1)S(1)}, bf16[1024,128]{1,0:T(8,128)(2,1)S(1)}, bf16[102...) while((s32[]{:T(128)}, ...), condition=%wide.region_6.6_spmd, body=%wide.region_1.5_spmd.sunk | while | flops 545588224 | bytes 15634557 | solution.py:49
  113.8 0.5 multiply_reduce_fusion.4
  114.3 0.5 multiply_reduce_fusion.5
  114.8 1.0 fusion.50
  115.8 0.5 convolution_multiply_fusion.3
  116.7 0.6 fusion.51
  117.3 0.5 multiply_reduce_fusion.4
  117.8 0.5 multiply_reduce_fusion.5
  118.4 1.0 fusion.50
  119.3 0.5 convolution_multiply_fusion.3
  120.3 0.6 fusion.51
  120.9 0.7 bitcast_dynamic-update-slice_fusion.2
  121.6 1.8 %copy.35 = bf16[3,1024,128]{2,0,1:T(4,128)(2,1)S(1)} copy(bf16[3,1024,128]{2,1,0:T(8,128)(2,1)} %get-tuple-element.79) | data formatting | bytes 1572864 | tf_op jit(solution)/shard_map/while | solution.py:64
  123.4 30.8 %all_to_all.60 = bf16[1024,1,3,128]{3,2,1,0:T(4,128)(2,1)S(1)} all-to-all(bf16[1024,1,3,128]{3,2,1,0:T(4,128)(2,1)S(1)} %bitcast.116), channel_id=1, replica_groups=mesh['seq'=16,'blk'=2] {'seq'}, dimensions={0} | all-to-all | bytes 1572864 | tf_op jit(solution)/shard_map/all_to_all | solution.py:67
  154.4 0.9 copy_bitcast_fusion.1
  (36 shorter events, 3.2 us)
Async XLA Ops:
  0.0 1.1 copy-start
  0.0 10.6 %copy-start.3 = (bf16[64,5120]{1,0:T(8,128)(2,1)S(1)}, bf16[64,5120]{1,0:T(8,128)(2,1)}, u32[]{:S(2)}) copy-start(bf16[64,5120]{1,0:T(8,128)(2,1)} %param.9) | copy-start | bytes 1966084
  2.2 28.0 %all-to-all-start.1 = ((bf16[64,16,3,128]{3,0,2,1:T(8,128)(2,1)}), bf16[64,16,3,128]{3,0,2,1:T(8,128)(2,1)S(1)}, u32[]{:S(2)}, u32[]{:S(2)}) async-start(bf16[64,16,3,128]{3,0,2,1:T(8,128)(2,1)} %bitcast.13), calls=%async_computation.1 | async-start | bytes 1572864 | tf_op jit(solution)/shard_map/all_to_all | solution.py:87
  30.3 23.6 %all-to-all-start.2 = ((bf16[64,16,3,128]{3,0,2,1:T(8,128)(2,1)}), bf16[64,16,3,128]{3,0,2,1:T(8,128)(2,1)S(1)}, u32[]{:S(2)}, u32[]{:S(2)}) async-start(bf16[64,16,3,128]{3,0,2,1:T(8,128)(2,1)} %bitcast.18), calls=%async_computation.2 | async-start | bytes 1572864 | tf_op jit(solution)/shard_map/all_to_all | solution.py:88
  53.9 0.9 copy-start.2
  54.8 2.6 %copy-start.4 = (bf16[64,5120]{1,0:T(8,128)(2,1)S(1)}, bf16[64,5120]{1,0:T(8,128)(2,1)}, u32[]{:S(2)}) copy-start(bf16[64,5120]{1,0:T(8,128)(2,1)} %param.7) | copy-start | bytes 1966084
  57.3 27.2 %collective-permute-start = (bf16[2,3,1024,128]{3,2,1,0:T(8,128)(2,1)}, bf16[2,3,1024,128]{3,2,1,0:T(8,128)(2,1)}, u32[]{:S(2)}, u32[]{:S(2)}) collective-permute-start(bf16[2,3,1024,128]{3,2,1,0:T(8,128)(2,1)} %pad_maximum_fusion), channel_id=1, source_target_pairs={{0,1},{1,0},{2,3},{3,2},{4,5},{5,4},{6,7},{7,6},{8,9},{9,8},{10,11... | collective-permute-start | bytes 4718600 | tf_op jit(solution)/shard_map/ppermute | solution.py:12
  58.5 25.1 %all-to-all-start = ((bf16[64,16,3,128]{3,0,2,1:T(8,128)(2,1)}), bf16[64,16,3,128]{3,0,2,1:T(8,128)(2,1)S(1)}, u32[]{:S(2)}, u32[]{:S(2)}) async-start(bf16[64,16,3,128]{3,0,2,1:T(8,128)(2,1)} %bitcast.121), calls=%async_computation | async-start | bytes 1572864 | tf_op jit(solution)/shard_map/all_to_all | solution.py:86
  92.8 1.0 copy-start.1
  96.3 1.0 copy-start.1
  104.3 1.0 copy-start.1
  107.8 1.0 copy-start.1
  115.8 1.0 copy-start.1
  119.3 1.0 copy-start.1
where the time goes:
time: 156 us; the launch traced here: 155 us
  waiting for transfers between devices  57.1 us (37%)
  blocking collectives  30.8 us (20%)
  local copies, waits for them, and re-layouts  28.7 us (18%)
  starting transfers between devices  18.2 us (12%)
  matrix products  12.9 us (8%)
  other arithmetic  7.11 us (5%)
    all_to_all x1, blocking collectives, attend_items(): lax.all_to_all(outcome, 'seq', split_axis=0, concat_axis=1, tiled=True)  30.8 us
    all_to_all x1, waiting for transfers between devices, on_device(): lax.all_to_all(split_heads(query), 'seq', split_axis=1, concat_axis=0, ti...  20.1 us
    all_to_all x1, waiting for transfers between devices, on_device(): lax.all_to_all(split_heads(value_source), 'seq', split_axis=1, concat_axi...  18.6 us
    all_to_all x1, waiting for transfers between devices, on_device(): lax.all_to_all(split_heads(key_source), 'seq', split_axis=1, concat_axis=...  18.5 us
    all_to_all x1, starting transfers between devices, on_device(): lax.all_to_all(split_heads(key_source), 'seq', split_axis=1, concat_axis=...  8.34 us
    squeeze x6, local copies, waits for them, and re-layouts, attend_items(): outcome = lax.map(attend_item, tiles)  8.03 us
    dot_general x12, matrix products, partial_block(): jnp.dot(expo.astype(jnp.bfloat16), v_tile, preferred_element_type=jnp.flo...  6.67 us
    dot_general x12, matrix products, partial_block(): lax.dot_general(q_rows, k_tile, (((1,), (1,)), ((), ())), preferred_eleme...  6.23 us
  transfers between devices with their start and end apart: 4, of which 3 were waited for; matrix products, arithmetic and copies ran while one was open for 2% of the time, Pallas kernels for 0%

commit v1 on v0

--- a/solution.py
+++ b/solution.py
@@ -68,6 +68,29 @@
 
 
 def on_device(query, keys, values):
+
+    def _see_forms(piece_in):
+        comm_axis = "seq"
+        x_new = jax.lax.axis_size(comm_axis)
+        small = jax.lax.axis_index(comm_axis)
+        spare, last = (x_new, small)
+        k_now = piece_in.shape[1] // spare
+        reached = list(piece_in.shape)
+        reached[1] = k_now
+        extra = reached[0]
+        reached[0] = extra * spare
+        item_now = jnp.zeros(reached, piece_in.dtype)
+        for pp in range(spare):
+            frame_out = lax.dynamic_slice_in_dim(piece_in, (last ^ pp) * k_now, k_now, axis=1)
+            if pp:
+                frame_out = jax.lax.ppermute(
+                    frame_out, axis_name=comm_axis, perm=[(rr, rr ^ pp) for rr in range(spare)]
+                )
+            item_now = lax.dynamic_update_slice_in_dim(
+                item_now, frame_out, (last ^ pp) * extra, axis=0
+            )
+        return item_now
+
     groups = lax.axis_size("seq")
     width = query.shape[1] // HEADS
     tok_rows = query.shape[0]
@@ -83,7 +106,7 @@
 
     result = attend_items(
         (
-            lax.all_to_all(split_heads(query), "seq", split_axis=1, concat_axis=0, tiled=True),
+            _see_forms(split_heads(query)),
             lax.all_to_all(split_heads(key_source), "seq", split_axis=1, concat_axis=0, tiled=True),
             lax.all_to_all(
                 split_heads(value_source), "seq", split_axis=1, concat_axis=0, tiled=True

time: 156 us -> 146 us (0.936)
  waiting for transfers between devices: 57.1 us -> 16 us
  starting transfers between devices: 18.2 us -> 41.4 us
  local copies, waits for them, and re-layouts: 28.7 us -> 39.6 us
  blocking collectives: 30.8 us -> 28.4 us
    ppermute x0 -> x15, starting transfers between devices: none -> 27.9 us  [_see_forms(): jax.lax.ppermute(frame_out, axis_name=comm_axis, perm=[(rr, rr ^ pp) for...]
    all_to_all x1 -> x0, waiting for transfers between devices: 20.1 us -> none  [on_device(): lax.all_to_all(split_heads(query), 'seq', split_axis=1, concat_axis=0, ti...]
    all_to_all x1, waiting for transfers between devices: 18.6 us -> 0.01 us  [on_device(): lax.all_to_all(split_heads(value_source), 'seq', split_axis=1, concat_axi...]
    dynamic_update_slice x0 -> x16, local copies, waits for them, and re-layouts: none -> 14.1 us  [_see_forms(): lax.dynamic_update_slice_in_dim(item_now, frame_out, (last ^ pp) * extra,...]
    all_to_all x1, waiting for transfers between devices: 18.5 us -> 4.44 us  [on_device(): lax.all_to_all(split_heads(key_source), 'seq', split_axis=1, concat_axis=...]
    ppermute x0 -> x15, waiting for transfers between devices: none -> 11.6 us  [_see_forms(): jax.lax.ppermute(frame_out, axis_name=comm_axis, perm=[(rr, rr ^ pp) for...]
    all_to_all x1 -> x0, starting transfers between devices: 4.95 us -> none  [on_device(): lax.all_to_all(split_heads(query), 'seq', split_axis=1, concat_axis=0, ti...]
    all_to_all x1, blocking collectives: 30.8 us -> 28.4 us  [attend_items(): lax.all_to_all(outcome, 'seq', split_axis=0, concat_axis=1, tiled=True)]
  transfers between devices with their start and end apart: 4 -> 18, of which waited for: 3 -> 3; matrix products, arithmetic and copies ran while one was open for 2% -> 12% of each run, Pallas kernels for 0% -> 0%
where the time goes in v1:
time: 146 us; the launch traced here: 145 us
  starting transfers between devices  41.4 us (28%)
  local copies, waits for them, and re-layouts  39.6 us (27%)
  blocking collectives  28.4 us (19%)
  waiting for transfers between devices  16 us (11%)
  matrix products  12.9 us (9%)
  other arithmetic  6.02 us (4%)
    all_to_all x1, blocking collectives, attend_items(): lax.all_to_all(outcome, 'seq', split_axis=0, concat_axis=1, tiled=True)  28.4 us
    ppermute x15, starting transfers between devices, _see_forms(): jax.lax.ppermute(frame_out, axis_name=comm_axis, perm=[(rr, rr ^ pp) for...  27.9 us
    dynamic_update_slice x16, local copies, waits for them, and re-layouts, _see_forms(): lax.dynamic_update_slice_in_dim(item_now, frame_out, (last ^ pp) * extra,...  14.1 us
    ppermute x15, waiting for transfers between devices, _see_forms(): jax.lax.ppermute(frame_out, axis_name=comm_axis, perm=[(rr, rr ^ pp) for...  11.6 us
    all_to_all x1, starting transfers between devices, on_device(): lax.all_to_all(split_heads(key_source), 'seq', split_axis=1, concat_axis=...  8.34 us
    squeeze x6, local copies, waits for them, and re-layouts, attend_items(): outcome = lax.map(attend_item, tiles)  8.03 us
    dot_general x12, matrix products, partial_block(): jnp.dot(expo.astype(jnp.bfloat16), v_tile, preferred_element_type=jnp.flo...  6.66 us
    dot_general x12, matrix products, partial_block(): lax.dot_general(q_rows, k_tile, (((1,), (1,)), ((), ())), preferred_eleme...  6.23 us
  transfers between devices with their start and end apart: 18, of which 3 were waited for; matrix products, arithmetic and copies ran while one was open for 12% of the time, Pallas kernels for 0%

profile of v1, /device:TPU:0, one launch (start us, length us, event | category | flops | bytes accessed | tf_op | source)
XLA Modules:
  0.0 145.0 jit_solution(9687961356207367418)
XLA Ops:
  0.0 1.1 copy-done
  1.3 1.0 pad.11.clone
  2.3 8.3 %all-to-all-start = ((bf16[64,16,3,128]{3,0,2,1:T(8,128)(2,1)}), bf16[64,16,3,128]{3,0,2,1:T(8,128)(2,1)S(1)}, u32[]{:S(2)}, u32[]{:S(2)}) async-start(bf16[64,16,3,128]{3,0,2,1:T(8,128)(2,1)} %bitcast.26), calls=%async_computation | async-start | bytes 1572864 | tf_op jit(solution)/shard_map/all_to_all | solution.py:110
  11.1 0.9 constant_dynamic-slice_fusion.1
  12.0 1.9 %collective-permute-start = (bf16[64,1,3,128]{3,0,2,1:T(8,128)(2,1)}, bf16[64,1,3,128]{3,0,2,1:T(8,128)(2,1)}, u32[]{:S(2)}, u32[]{:S(2)}) collective-permute-start(bf16[64,1,3,128]{3,0,2,1:T(8,128)(2,1)} %get-tuple-element.137), channel_id=1, source_target_pairs={{0,2},{2,0},{4,6},{6,4},{8,10},{10,8},{12,14},{14,12},{16,18},{18,... | collective-permute-start | bytes 147464 | tf_op jit(solution)/shard_map/ppermute | solution.py:86
  13.9 1.5 %collective-permute-start.1 = (bf16[64,1,3,128]{3,0,2,1:T(8,128)(2,1)}, bf16[64,1,3,128]{3,0,2,1:T(8,128)(2,1)}, u32[]{:S(2)}, u32[]{:S(2)}) collective-permute-start(bf16[64,1,3,128]{3,0,2,1:T(8,128)(2,1)} %get-tuple-element.136), channel_id=1, source_target_pairs={{0,4},{2,6},{4,0},{6,2},{8,12},{10,14},{12,8},{14,10},{16,20},{18,... | collective-permute-start | bytes 147464 | tf_op jit(solution)/shard_map/ppermute | solution.py:86
  15.5 1.9 %collective-permute-start.3 = (bf16[64,1,3,128]{3,0,2,1:T(8,128)(2,1)}, bf16[64,1,3,128]{3,0,2,1:T(8,128)(2,1)}, u32[]{:S(2)}, u32[]{:S(2)}) collective-permute-start(bf16[64,1,3,128]{3,0,2,1:T(8,128)(2,1)} %get-tuple-element.134), channel_id=1, source_target_pairs={{0,8},{2,10},{4,12},{6,14},{8,0},{10,2},{12,4},{14,6},{16,24},{18,... | collective-permute-start | bytes 147464 | tf_op jit(solution)/shard_map/ppermute | solution.py:86
  17.4 1.5 %collective-permute-start.4 = (bf16[64,1,3,128]{3,0,2,1:T(8,128)(2,1)}, bf16[64,1,3,128]{3,0,2,1:T(8,128)(2,1)}, u32[]{:S(2)}, u32[]{:S(2)}) collective-permute-start(bf16[64,1,3,128]{3,0,2,1:T(8,128)(2,1)} %get-tuple-element.133), channel_id=1, source_target_pairs={{0,10},{2,8},{4,14},{6,12},{8,2},{10,0},{12,6},{14,4},{16,26},{18,... | collective-permute-start | bytes 147464 | tf_op jit(solution)/shard_map/ppermute | solution.py:86
  19.1 1.0 reshape.135
  20.1 0.6 bitcast_dynamic-update-slice_fusion.16
  20.7 1.0 pad.12.clone
  21.8 2.4 %collective-permute-start.5 = (bf16[64,1,3,128]{3,0,2,1:T(8,128)(2,1)S(1)}, bf16[64,1,3,128]{3,0,2,1:T(8,128)(2,1)S(1)}, u32[]{:S(2)}, u32[]{:S(2)}) collective-permute-start(bf16[64,1,3,128]{3,0,2,1:T(8,128)(2,1)S(1)} %copy-done.13), channel_id=1, source_target_pairs={{0,12},{2,14},{4,8},{6,10},{8,4},{10,6},{12,0},{14,2},{16,28},{18,... | collective-permute-start | bytes 147464 | tf_op jit(solution)/shard_map/ppermute | solution.py:86
  24.1 1.4 bitcast_dynamic-update-slice_fusion.15
  25.7 4.4 %all-to-all-done = bf16[64,16,3,128]{3,0,2,1:T(8,128)(2,1)S(1)} async-done(((bf16[64,16,3,128]{3,0,2,1:T(8,128)(2,1)}), bf16[64,16,3,128]{3,0,2,1:T(8,128)(2,1)S(1)}, u32[]{:S(2)}, u32[]{:S(2)}) %all-to-all-start) | async-done | bytes 786464 | tf_op jit(solution)/shard_map/all_to_all | solution.py:110
  30.2 5.1 %all-to-all-start.1 = ((bf16[64,16,3,128]{3,0,2,1:T(8,128)(2,1)}), bf16[64,16,3,128]{3,0,2,1:T(8,128)(2,1)S(1)}, u32[]{:S(2)}, u32[]{:S(2)}) async-start(bf16[64,16,3,128]{3,0,2,1:T(8,128)(2,1)} %bitcast.31), calls=%async_computation.1 | async-start | bytes 1572864 | tf_op jit(solution)/shard_map/all_to_all | solution.py:111
  35.3 1.4 bitcast_dynamic-update-slice_fusion.14
  36.7 2.8 %collective-permute-start.7 = (bf16[64,1,3,128]{3,0,2,1:T(8,128)(2,1)S(1)}, bf16[64,1,3,128]{3,0,2,1:T(8,128)(2,1)S(1)}, u32[]{:S(2)}, u32[]{:S(2)}) collective-permute-start(bf16[64,1,3,128]{3,0,2,1:T(8,128)(2,1)S(1)} %copy-done.11), channel_id=1, source_target_pairs={{0,16},{2,18},{4,20},{6,22},{8,24},{10,26},{12,28},{14,30},{16,0},... | collective-permute-start | bytes 147464 | tf_op jit(solution)/shard_map/ppermute | solution.py:86
  39.6 1.4 bitcast_dynamic-update-slice_fusion.13
  41.0 1.5 %collective-permute-start.8 = (bf16[64,1,3,128]{3,0,2,1:T(8,128)(2,1)S(1)}, bf16[64,1,3,128]{3,0,2,1:T(8,128)(2,1)S(1)}, u32[]{:S(2)}, u32[]{:S(2)}) collective-permute-start(bf16[64,1,3,128]{3,0,2,1:T(8,128)(2,1)S(1)} %copy-done.10), channel_id=1, source_target_pairs={{0,18},{2,16},{4,22},{6,20},{8,26},{10,24},{12,30},{14,28},{16,2},... | collective-permute-start | bytes 147464 | tf_op jit(solution)/shard_map/ppermute | solution.py:86
  42.5 1.4 bitcast_dynamic-update-slice_fusion.12
  43.9 3.3 %collective-permute-start.9 = (bf16[64,1,3,128]{3,0,2,1:T(8,128)(2,1)S(1)}, bf16[64,1,3,128]{3,0,2,1:T(8,128)(2,1)S(1)}, u32[]{:S(2)}, u32[]{:S(2)}) collective-permute-start(bf16[64,1,3,128]{3,0,2,1:T(8,128)(2,1)S(1)} %copy-done.9), channel_id=1, source_target_pairs={{0,20},{2,22},{4,16},{6,18},{8,28},{10,30},{12,24},{14,26},{16,4},... | collective-permute-start | bytes 147464 | tf_op jit(solution)/shard_map/ppermute | solution.py:86
  47.2 1.4 bitcast_dynamic-update-slice_fusion.11
  48.7 0.6 bitcast_dynamic-update-slice_fusion.10
  49.3 3.7 %collective-permute-start.11 = (bf16[64,1,3,128]{3,0,2,1:T(8,128)(2,1)S(1)}, bf16[64,1,3,128]{3,0,2,1:T(8,128)(2,1)S(1)}, u32[]{:S(2)}, u32[]{:S(2)}) collective-permute-start(bf16[64,1,3,128]{3,0,2,1:T(8,128)(2,1)S(1)} %copy-done.7), channel_id=1, source_target_pairs={{0,24},{2,26},{4,28},{6,30},{8,16},{10,18},{12,20},{14,22},{16,8},... | collective-permute-start | bytes 147464 | tf_op jit(solution)/shard_map/ppermute | solution.py:86
  53.1 0.6 bitcast_dynamic-update-slice_fusion.9
  53.7 7.9 %collective-permute-done.7 = bf16[64,1,3,128]{3,0,2,1:T(8,128)(2,1)S(1)} collective-permute-done((bf16[64,1,3,128]{3,0,2,1:T(8,128)(2,1)S(1)}, bf16[64,1,3,128]{3,0,2,1:T(8,128)(2,1)S(1)}, u32[]{:S(2)}, u32[]{:S(2)}) %collective-permute-start.7) | collective-permute-done | bytes 49184 | tf_op jit(solution)/shard_map/ppermute | solution.py:86
  61.6 2.5 %collective-permute-start.12 = (bf16[64,1,3,128]{3,0,2,1:T(8,128)(2,1)S(1)}, bf16[64,1,3,128]{3,0,2,1:T(8,128)(2,1)S(1)}, u32[]{:S(2)}, u32[]{:S(2)}) collective-permute-start(bf16[64,1,3,128]{3,0,2,1:T(8,128)(2,1)S(1)} %copy-done.6), channel_id=1, source_target_pairs={{0,26},{2,24},{4,30},{6,28},{8,18},{10,16},{12,22},{14,20},{16,10}... | collective-permute-start | bytes 147464 | tf_op jit(solution)/shard_map/ppermute | solution.py:86
  64.1 0.6 bitcast_dynamic-update-slice_fusion.8
  65.1 0.6 bitcast_dynamic-update-slice_fusion.7
  65.8 3.1 %collective-permute-start.13 = (bf16[64,1,3,128]{3,0,2,1:T(8,128)(2,1)S(1)}, bf16[64,1,3,128]{3,0,2,1:T(8,128)(2,1)S(1)}, u32[]{:S(2)}, u32[]{:S(2)}) collective-permute-start(bf16[64,1,3,128]{3,0,2,1:T(8,128)(2,1)S(1)} %copy-done.5), channel_id=1, source_target_pairs={{0,28},{2,30},{4,24},{6,26},{8,20},{10,22},{12,16},{14,18},{16,12}... | collective-permute-start | bytes 147464 | tf_op jit(solution)/shard_map/ppermute | solution.py:86
  68.9 0.6 bitcast_dynamic-update-slice_fusion.6
  69.5 1.5 %collective-permute-start.14 = (bf16[64,1,3,128]{3,0,2,1:T(8,128)(2,1)S(1)}, bf16[64,1,3,128]{3,0,2,1:T(8,128)(2,1)S(1)}, u32[]{:S(2)}, u32[]{:S(2)}) collective-permute-start(bf16[64,1,3,128]{3,0,2,1:T(8,128)(2,1)S(1)} %copy-done.4), channel_id=1, source_target_pairs={{0,30},{2,28},{4,26},{6,24},{8,22},{10,20},{12,18},{14,16},{16,14}... | collective-permute-start | bytes 147464 | tf_op jit(solution)/shard_map/ppermute | solution.py:86
  71.1 0.6 bitcast_dynamic-update-slice_fusion.5
  71.7 0.6 bitcast_dynamic-update-slice_fusion.4
  72.3 0.6 bitcast_dynamic-update-slice_fusion.3
  72.9 0.6 bitcast_dynamic-update-slice_fusion.2
  73.6 3.7 %collective-permute-done.14 = bf16[64,1,3,128]{3,0,2,1:T(8,128)(2,1)S(1)} collective-permute-done((bf16[64,1,3,128]{3,0,2,1:T(8,128)(2,1)S(1)}, bf16[64,1,3,128]{3,0,2,1:T(8,128)(2,1)S(1)}, u32[]{:S(2)}, u32[]{:S(2)}) %collective-permute-start.14) | collective-permute-done | bytes 49184 | tf_op jit(solution)/shard_map/ppermute | solution.py:86
  77.2 0.6 bitcast_dynamic-update-slice_fusion.1
  77.9 1.3 slice_bitcast_fusion
  79.1 34.6 %while.21 = (s32[]{:T(128)}, bf16[3,1024,128]{2,1,0:T(8,128)(2,1)}, bf16[3,1024,128]{2,1,0:T(8,128)(2,1)}, bf16[3,1024,128]{2,1,0:T(8,128)(2,1)S(1)}, bf16[3,102...) while((s32[]{:T(128)}, bf16[3,1024,128]{2,1,0:T(8,128)(2,1)}, ...), condition=%wide.region_7.8_spmd, body=%wide.region_0.7_spmd.sunk | while | flops 545588224 | bytes 18780980 | solution.py:64
  79.1 1.0 dynamic-slice_bitcast_fusion.6
  80.1 1.7 %dynamic-slice_bitcast_fusion.7 = (bf16[1024,128]{1,0:T(8,128)(2,1)}, bf16[1024,128]{1,0:T(8,128)(2,1)S(1)}) fusion(bf16[3,1024,128]{2,1,0:T(8,128)(2,1)} %get-tuple-element.317, s32[]{:T(128)} %get-tuple-element.301, bf16[3,1024,128]{2,1,0:T(8,128)(2,1)S(1)} %get-tuple-element.315), kind=kLoop, calls=%fused_computation.35.clone.1 | loop fusion | bytes 1048580 | tf_op jit(solution)/shard_map/while/body/jit(dynamic_index_in_dim)/squeeze | solution.py:64
  81.8 1.0 constant_dynamic-slice_fusion.17
  82.8 7.1 %while.22 = (s32[]{:T(128)}, bf16[2,512,128]{2,1,0:T(8,128)(2,1)S(1)}, bf16[2,512,128]{2,1,0:T(8,128)(2,1)S(1)}, bf16[1024,128]{1,0:T(8,128)(2,1)S(1)}, bf16[102...) while((s32[]{:T(128)}, ...), condition=%wide.region_6.6_spmd, body=%wide.region_1.5_spmd.sunk | while | flops 545588224 | bytes 15634557 | solution.py:49
  83.8 1.0 fusion.50
  87.4 1.0 fusion.50
  89.9 0.7 bitcast_dynamic-update-slice_fusion.18
  90.6 1.0 dynamic-slice_bitcast_fusion.6
  91.6 1.7 %dynamic-slice_bitcast_fusion.7 = (bf16[1024,128]{1,0:T(8,128)(2,1)}, bf16[1024,128]{1,0:T(8,128)(2,1)S(1)}) fusion(bf16[3,1024,128]{2,1,0:T(8,128)(2,1)} %get-tuple-element.317, s32[]{:T(128)} %get-tuple-element.301, bf16[3,1024,128]{2,1,0:T(8,128)(2,1)S(1)} %get-tuple-element.315), kind=kLoop, calls=%fused_computation.35.clone.1 | loop fusion | bytes 1048580 | tf_op jit(solution)/shard_map/while/body/jit(dynamic_index_in_dim)/squeeze | solution.py:64
  93.3 1.0 constant_dynamic-slice_fusion.17
  94.3 7.1 %while.22 = (s32[]{:T(128)}, bf16[2,512,128]{2,1,0:T(8,128)(2,1)S(1)}, bf16[2,512,128]{2,1,0:T(8,128)(2,1)S(1)}, bf16[1024,128]{1,0:T(8,128)(2,1)S(1)}, bf16[102...) while((s32[]{:T(128)}, ...), condition=%wide.region_6.6_spmd, body=%wide.region_1.5_spmd.sunk | while | flops 545588224 | bytes 15634557 | solution.py:49
  95.3 1.0 fusion.50
  98.9 1.0 fusion.50
  101.4 0.7 bitcast_dynamic-update-slice_fusion.18
  102.2 1.0 dynamic-slice_bitcast_fusion.6
  103.1 1.7 %dynamic-slice_bitcast_fusion.7 = (bf16[1024,128]{1,0:T(8,128)(2,1)}, bf16[1024,128]{1,0:T(8,128)(2,1)S(1)}) fusion(bf16[3,1024,128]{2,1,0:T(8,128)(2,1)} %get-tuple-element.317, s32[]{:T(128)} %get-tuple-element.301, bf16[3,1024,128]{2,1,0:T(8,128)(2,1)S(1)} %get-tuple-element.315), kind=kLoop, calls=%fused_computation.35.clone.1 | loop fusion | bytes 1048580 | tf_op jit(solution)/shard_map/while/body/jit(dynamic_index_in_dim)/squeeze | solution.py:64
  104.8 1.0 constant_dynamic-slice_fusion.17
  105.8 7.1 %while.22 = (s32[]{:T(128)}, bf16[2,512,128]{2,1,0:T(8,128)(2,1)S(1)}, bf16[2,512,128]{2,1,0:T(8,128)(2,1)S(1)}, bf16[1024,128]{1,0:T(8,128)(2,1)S(1)}, bf16[102...) while((s32[]{:T(128)}, ...), condition=%wide.region_6.6_spmd, body=%wide.region_1.5_spmd.sunk | while | flops 545588224 | bytes 15634557 | solution.py:49
  106.9 1.0 fusion.50
  110.4 1.0 fusion.50
  112.9 0.7 bitcast_dynamic-update-slice_fusion.18
  113.7 1.8 %copy.34 = bf16[3,1024,128]{2,0,1:T(4,128)(2,1)S(1)} copy(bf16[3,1024,128]{2,1,0:T(8,128)(2,1)} %get-tuple-element.79) | data formatting | bytes 1572864 | tf_op jit(solution)/shard_map/while | solution.py:64
  115.5 28.4 %all_to_all.45 = bf16[1024,1,3,128]{3,2,1,0:T(4,128)(2,1)S(1)} all-to-all(bf16[1024,1,3,128]{3,2,1,0:T(4,128)(2,1)S(1)} %bitcast.142), channel_id=1, replica_groups=mesh['seq'=16,'blk'=2] {'seq'}, dimensions={0} | all-to-all | bytes 1572864 | tf_op jit(solution)/shard_map/all_to_all | solution.py:67
  144.1 0.9 copy_bitcast_fusion.1
  (99 shorter events, 17.0 us)
Async XLA Ops:
  0.0 1.1 copy-start
  0.0 10.7 %copy-start.2 = (bf16[64,5120]{1,0:T(8,128)(2,1)S(1)}, bf16[64,5120]{1,0:T(8,128)(2,1)}, u32[]{:S(2)}) copy-start(bf16[64,5120]{1,0:T(8,128)(2,1)} %param.7) | copy-start | bytes 1966084
  2.3 27.9 %all-to-all-start = ((bf16[64,16,3,128]{3,0,2,1:T(8,128)(2,1)}), bf16[64,16,3,128]{3,0,2,1:T(8,128)(2,1)S(1)}, u32[]{:S(2)}, u32[]{:S(2)}) async-start(bf16[64,16,3,128]{3,0,2,1:T(8,128)(2,1)} %bitcast.26), calls=%async_computation | async-start | bytes 1572864 | tf_op jit(solution)/shard_map/all_to_all | solution.py:110
  10.7 8.1 %copy-start.3 = (bf16[64,5120]{1,0:T(8,128)(2,1)S(1)}, bf16[64,5120]{1,0:T(8,128)(2,1)}, u32[]{:S(2)}) copy-start(bf16[64,5120]{1,0:T(8,128)(2,1)} %param.9) | copy-start | bytes 1966084
  12.0 9.7 %collective-permute-start = (bf16[64,1,3,128]{3,0,2,1:T(8,128)(2,1)}, bf16[64,1,3,128]{3,0,2,1:T(8,128)(2,1)}, u32[]{:S(2)}, u32[]{:S(2)}) collective-permute-start(bf16[64,1,3,128]{3,0,2,1:T(8,128)(2,1)} %get-tuple-element.137), channel_id=1, source_target_pairs={{0,2},{2,0},{4,6},{6,4},{8,10},{10,8},{12,14},{14,12},{16,18},{18,... | collective-permute-start | bytes 147464 | tf_op jit(solution)/shard_map/ppermute | solution.py:86
  13.9 11.7 %collective-permute-start.1 = (bf16[64,1,3,128]{3,0,2,1:T(8,128)(2,1)}, bf16[64,1,3,128]{3,0,2,1:T(8,128)(2,1)}, u32[]{:S(2)}, u32[]{:S(2)}) collective-permute-start(bf16[64,1,3,128]{3,0,2,1:T(8,128)(2,1)} %get-tuple-element.136), channel_id=1, source_target_pairs={{0,4},{2,6},{4,0},{6,2},{8,12},{10,14},{12,8},{14,10},{16,20},{18,... | collective-permute-start | bytes 147464 | tf_op jit(solution)/shard_map/ppermute | solution.py:86
  15.4 21.4 %collective-permute-start.2 = (bf16[64,1,3,128]{3,0,2,1:T(8,128)(2,1)}, bf16[64,1,3,128]{3,0,2,1:T(8,128)(2,1)}, u32[]{:S(2)}, u32[]{:S(2)}) collective-permute-start(bf16[64,1,3,128]{3,0,2,1:T(8,128)(2,1)} %get-tuple-element.135), channel_id=1, source_target_pairs={{0,6},{2,4},{4,2},{6,0},{8,14},{10,12},{12,10},{14,8},{16,22},{18,... | collective-permute-start | bytes 147464 | tf_op jit(solution)/shard_map/ppermute | solution.py:86
  15.5 25.5 %collective-permute-start.3 = (bf16[64,1,3,128]{3,0,2,1:T(8,128)(2,1)}, bf16[64,1,3,128]{3,0,2,1:T(8,128)(2,1)}, u32[]{:S(2)}, u32[]{:S(2)}) collective-permute-start(bf16[64,1,3,128]{3,0,2,1:T(8,128)(2,1)} %get-tuple-element.134), channel_id=1, source_target_pairs={{0,8},{2,10},{4,12},{6,14},{8,0},{10,2},{12,4},{14,6},{16,24},{18,... | collective-permute-start | bytes 147464 | tf_op jit(solution)/shard_map/ppermute | solution.py:86
  17.4 26.5 %collective-permute-start.4 = (bf16[64,1,3,128]{3,0,2,1:T(8,128)(2,1)}, bf16[64,1,3,128]{3,0,2,1:T(8,128)(2,1)}, u32[]{:S(2)}, u32[]{:S(2)}) collective-permute-start(bf16[64,1,3,128]{3,0,2,1:T(8,128)(2,1)} %get-tuple-element.133), channel_id=1, source_target_pairs={{0,10},{2,8},{4,14},{6,12},{8,2},{10,0},{12,6},{14,4},{16,26},{18,... | collective-permute-start | bytes 147464 | tf_op jit(solution)/shard_map/ppermute | solution.py:86
  19.0 2.7 %copy-start.13 = (bf16[64,1,3,128]{3,0,2,1:T(8,128)(2,1)S(1)}, bf16[64,1,3,128]{3,0,2,1:T(8,128)(2,1)}, u32[]{:S(2)}) copy-start(bf16[64,1,3,128]{3,0,2,1:T(8,128)(2,1)} %get-tuple-element.132) | copy-start | bytes 147460
  19.1 6.5 %copy-start.12 = (bf16[64,1,3,128]{3,0,2,1:T(8,128)(2,1)S(1)}, bf16[64,1,3,128]{3,0,2,1:T(8,128)(2,1)}, u32[]{:S(2)}) copy-start(bf16[64,1,3,128]{3,0,2,1:T(8,128)(2,1)} %get-tuple-element.131) | copy-start | bytes 147460
  19.1 17.7 %copy-start.11 = (bf16[64,1,3,128]{3,0,2,1:T(8,128)(2,1)S(1)}, bf16[64,1,3,128]{3,0,2,1:T(8,128)(2,1)}, u32[]{:S(2)}) copy-start(bf16[64,1,3,128]{3,0,2,1:T(8,128)(2,1)} %get-tuple-element.130) | copy-start | bytes 147460
  19.1 21.9 %copy-start.10 = (bf16[64,1,3,128]{3,0,2,1:T(8,128)(2,1)S(1)}, bf16[64,1,3,128]{3,0,2,1:T(8,128)(2,1)}, u32[]{:S(2)}) copy-start(bf16[64,1,3,128]{3,0,2,1:T(8,128)(2,1)} %get-tuple-element.129) | copy-start | bytes 147460
  19.1 24.8 %copy-start.9 = (bf16[64,1,3,128]{3,0,2,1:T(8,128)(2,1)S(1)}, bf16[64,1,3,128]{3,0,2,1:T(8,128)(2,1)}, u32[]{:S(2)}) copy-start(bf16[64,1,3,128]{3,0,2,1:T(8,128)(2,1)} %get-tuple-element.128) | copy-start | bytes 147460
  19.1 29.5 %copy-start.8 = (bf16[64,1,3,128]{3,0,2,1:T(8,128)(2,1)S(1)}, bf16[64,1,3,128]{3,0,2,1:T(8,128)(2,1)}, u32[]{:S(2)}) copy-start(bf16[64,1,3,128]{3,0,2,1:T(8,128)(2,1)} %get-tuple-element.127) | copy-start | bytes 147460
  20.1 29.2 %copy-start.7 = (bf16[64,1,3,128]{3,0,2,1:T(8,128)(2,1)S(1)}, bf16[64,1,3,128]{3,0,2,1:T(8,128)(2,1)}, u32[]{:S(2)}) copy-start(bf16[64,1,3,128]{3,0,2,1:T(8,128)(2,1)} %get-tuple-element.126) | copy-start | bytes 147460
  20.1 41.5 %copy-start.6 = (bf16[64,1,3,128]{3,0,2,1:T(8,128)(2,1)S(1)}, bf16[64,1,3,128]{3,0,2,1:T(8,128)(2,1)}, u32[]{:S(2)}) copy-start(bf16[64,1,3,128]{3,0,2,1:T(8,128)(2,1)} %get-tuple-element.125) | copy-start | bytes 147460
  21.8 26.8 %collective-permute-start.5 = (bf16[64,1,3,128]{3,0,2,1:T(8,128)(2,1)S(1)}, bf16[64,1,3,128]{3,0,2,1:T(8,128)(2,1)S(1)}, u32[]{:S(2)}, u32[]{:S(2)}) collective-permute-start(bf16[64,1,3,128]{3,0,2,1:T(8,128)(2,1)S(1)} %copy-done.13), channel_id=1, source_target_pairs={{0,12},{2,14},{4,8},{6,10},{8,4},{10,6},{12,0},{14,2},{16,28},{18,... | collective-permute-start | bytes 147464 | tf_op jit(solution)/shard_map/ppermute | solution.py:86
  25.6 23.8 %collective-permute-start.6 = (bf16[64,1,3,128]{3,0,2,1:T(8,128)(2,1)S(1)}, bf16[64,1,3,128]{3,0,2,1:T(8,128)(2,1)S(1)}, u32[]{:S(2)}, u32[]{:S(2)}) collective-permute-start(bf16[64,1,3,128]{3,0,2,1:T(8,128)(2,1)S(1)} %copy-done.12), channel_id=1, source_target_pairs={{0,14},{2,12},{4,10},{6,8},{8,6},{10,4},{12,2},{14,0},{16,30},{18,... | collective-permute-start | bytes 147464 | tf_op jit(solution)/shard_map/ppermute | solution.py:86
  30.2 34.6 %all-to-all-start.1 = ((bf16[64,16,3,128]{3,0,2,1:T(8,128)(2,1)}), bf16[64,16,3,128]{3,0,2,1:T(8,128)(2,1)S(1)}, u32[]{:S(2)}, u32[]{:S(2)}) async-start(bf16[64,16,3,128]{3,0,2,1:T(8,128)(2,1)} %bitcast.31), calls=%async_computation.1 | async-start | bytes 1572864 | tf_op jit(solution)/shard_map/all_to_all | solution.py:111
  36.7 24.9 %collective-permute-start.7 = (bf16[64,1,3,128]{3,0,2,1:T(8,128)(2,1)S(1)}, bf16[64,1,3,128]{3,0,2,1:T(8,128)(2,1)S(1)}, u32[]{:S(2)}, u32[]{:S(2)}) collective-permute-start(bf16[64,1,3,128]{3,0,2,1:T(8,128)(2,1)S(1)} %copy-done.11), channel_id=1, source_target_pairs={{0,16},{2,18},{4,20},{6,22},{8,24},{10,26},{12,28},{14,30},{16,0},... | collective-permute-start | bytes 147464 | tf_op jit(solution)/shard_map/ppermute | solution.py:86
  41.0 24.0 %collective-permute-start.8 = (bf16[64,1,3,128]{3,0,2,1:T(8,128)(2,1)S(1)}, bf16[64,1,3,128]{3,0,2,1:T(8,128)(2,1)S(1)}, u32[]{:S(2)}, u32[]{:S(2)}) collective-permute-start(bf16[64,1,3,128]{3,0,2,1:T(8,128)(2,1)S(1)} %copy-done.10), channel_id=1, source_target_pairs={{0,18},{2,16},{4,22},{6,20},{8,26},{10,24},{12,30},{14,28},{16,2},... | collective-permute-start | bytes 147464 | tf_op jit(solution)/shard_map/ppermute | solution.py:86
  43.9 21.9 %collective-permute-start.9 = (bf16[64,1,3,128]{3,0,2,1:T(8,128)(2,1)S(1)}, bf16[64,1,3,128]{3,0,2,1:T(8,128)(2,1)S(1)}, u32[]{:S(2)}, u32[]{:S(2)}) collective-permute-start(bf16[64,1,3,128]{3,0,2,1:T(8,128)(2,1)S(1)} %copy-done.9), channel_id=1, source_target_pairs={{0,20},{2,22},{4,16},{6,18},{8,28},{10,30},{12,24},{14,26},{16,4},... | collective-permute-start | bytes 147464 | tf_op jit(solution)/shard_map/ppermute | solution.py:86
  48.6 21.0 %collective-permute-start.10 = (bf16[64,1,3,128]{3,0,2,1:T(8,128)(2,1)S(1)}, bf16[64,1,3,128]{3,0,2,1:T(8,128)(2,1)S(1)}, u32[]{:S(2)}, u32[]{:S(2)}) collective-permute-start(bf16[64,1,3,128]{3,0,2,1:T(8,128)(2,1)S(1)} %copy-done.8), channel_id=1, source_target_pairs={{0,22},{2,20},{4,18},{6,16},{8,30},{10,28},{12,26},{14,24},{16,6},... | collective-permute-start | bytes 147464 | tf_op jit(solution)/shard_map/ppermute | solution.py:86
  49.3 22.4 %collective-permute-start.11 = (bf16[64,1,3,128]{3,0,2,1:T(8,128)(2,1)S(1)}, bf16[64,1,3,128]{3,0,2,1:T(8,128)(2,1)S(1)}, u32[]{:S(2)}, u32[]{:S(2)}) collective-permute-start(bf16[64,1,3,128]{3,0,2,1:T(8,128)(2,1)S(1)} %copy-done.7), channel_id=1, source_target_pairs={{0,24},{2,26},{4,28},{6,30},{8,16},{10,18},{12,20},{14,22},{16,8},... | collective-permute-start | bytes 147464 | tf_op jit(solution)/shard_map/ppermute | solution.py:86
  61.6 10.7 %collective-permute-start.12 = (bf16[64,1,3,128]{3,0,2,1:T(8,128)(2,1)S(1)}, bf16[64,1,3,128]{3,0,2,1:T(8,128)(2,1)S(1)}, u32[]{:S(2)}, u32[]{:S(2)}) collective-permute-start(bf16[64,1,3,128]{3,0,2,1:T(8,128)(2,1)S(1)} %copy-done.6), channel_id=1, source_target_pairs={{0,26},{2,24},{4,30},{6,28},{8,18},{10,16},{12,22},{14,20},{16,10}... | collective-permute-start | bytes 147464 | tf_op jit(solution)/shard_map/ppermute | solution.py:86
  64.8 1.0 copy-start.5
  64.8 4.8 %copy-start.4 = (bf16[64,1,3,128]{3,0,2,1:T(8,128)(2,1)S(1)}, bf16[64,1,3,128]{3,0,2,1:T(8,128)(2,1)}, u32[]{:S(2)}) copy-start(bf16[64,1,3,128]{3,0,2,1:T(8,128)(2,1)} %get-tuple-element.123) | copy-start | bytes 147460
  65.0 12.8 %collective-permute-start.15 = (bf16[2,3,1024,128]{3,2,1,0:T(8,128)(2,1)S(1)}, bf16[2,3,1024,128]{3,2,1,0:T(8,128)(2,1)S(1)}, u32[]{:S(2)}, u32[]{:S(2)}) collective-permute-start(bf16[2,3,1024,128]{3,2,1,0:T(8,128)(2,1)S(1)} %pad_maximum_fusion), channel_id=1, source_target_pairs={{0,1},{1,0},{2,3},{3,2},{4,5},{5,4},{6,7},{7,6},{8,9},{9,8},{10,11... | collective-permute-start | bytes 4718600 | tf_op jit(solution)/shard_map/ppermute | solution.py:12
  65.8 7.2 %collective-permute-start.13 = (bf16[64,1,3,128]{3,0,2,1:T(8,128)(2,1)S(1)}, bf16[64,1,3,128]{3,0,2,1:T(8,128)(2,1)S(1)}, u32[]{:S(2)}, u32[]{:S(2)}) collective-permute-start(bf16[64,1,3,128]{3,0,2,1:T(8,128)(2,1)S(1)} %copy-done.5), channel_id=1, source_target_pairs={{0,28},{2,30},{4,24},{6,26},{8,20},{10,22},{12,16},{14,18},{16,12}... | collective-permute-start | bytes 147464 | tf_op jit(solution)/shard_map/ppermute | solution.py:86
  69.5 7.7 %collective-permute-start.14 = (bf16[64,1,3,128]{3,0,2,1:T(8,128)(2,1)S(1)}, bf16[64,1,3,128]{3,0,2,1:T(8,128)(2,1)S(1)}, u32[]{:S(2)}, u32[]{:S(2)}) collective-permute-start(bf16[64,1,3,128]{3,0,2,1:T(8,128)(2,1)S(1)} %copy-done.4), channel_id=1, source_target_pairs={{0,30},{2,28},{4,26},{6,24},{8,22},{10,20},{12,18},{14,16},{16,14}... | collective-permute-start | bytes 147464 | tf_op jit(solution)/shard_map/ppermute | solution.py:86
  84.8 1.0 copy-start.1
  88.4 1.0 copy-start.1
  96.3 1.0 copy-start.1
  99.9 1.0 copy-start.1
  107.8 1.0 copy-start.1
  111.4 1.0 copy-start.1
